TPU v7x, 256 devices: a whole 4x4x8 slice. The times are simulated.
256 devices in a mesh: freq: 16 (over z, core), tm: 16 (over y, x).
Axes of the slice: x: 4, y: 4, z: 8, core: 2. Of those that a mesh axis runs over, the one named last changes fastest.
Arguments:
- band_state: float32 [2048, 16384], P('freq', 'tm'), may hold values from -2.5 to 2.5
- lower_rows: int32 [3, 2048], replicated, may hold values from 0 to 2047, as said below
- upper_rows: int32 [3, 2048], replicated, may hold values from 0 to 2047, as said below
- delays: int32 [3, 2048], replicated, may hold values from 0 to 1024, as said below
- counts: int32 [7], replicated, may hold values from 256 to 2048, as said below
Outputs:
- dedispersed: float32 [2048, 16384], P('freq', 'tm')
Inputs may be any that keep to these rules, and one draw needn't show every extreme that they name: `counts`: entry 8 - 8 / 2^k + b is the live row count of output sub-band b of iteration k; it lies between half and all of that sub-band's 2 * 2048 / 2^(3 - k) padded rows, and in every iteration some sub-band has all its rows live. With w = 2048 / 2^(3 - k), lower_rows[k, i] is a row of input sub-band 2 * floor(i / (2 * w)) whose position in that sub-band is below its live count (all w rows are live in iteration 0). With w = 2048 / 2^(3 - k), upper_rows[k, i] is a row of input sub-band 2 * floor(i / (2 * w)) + 1 whose position in that sub-band is below its live count (all w rows are live in iteration 0). delays[k, i] is at most 2048 / 2^(3 - k), and equals it at some row in every iteration.
All inputs are finite; a program needn't handle non-finite values.
Results may differ from a plain program's by a relative error of at most 0.0003.
Values sent between devices are 32-bit elements; how exact they have to be, the bound alone decides.
A program may use at most 64 MiB of HBM per device.

v0:
```python
import jax
import jax.numpy as jnp
from jax import lax
from jax.sharding import PartitionSpec as P

DMAX = 2048
ITERS = 3


def shifted_2(block, axis, distance):
    devices = range(lax.axis_size(axis))
    route = [(i - distance, i) for i in devices if i - distance in devices]
    return lax.ppermute(block, axis, route)


def delay_columns(extended, shifts, widest):
    row_count = extended.shape[0]
    for bit_index in range(widest.bit_length()):
        stride = 1 << bit_index
        shifted = jnp.concatenate(
            [jnp.zeros((row_count, stride), extended.dtype), extended[:, :-stride]], axis=1
        )
        extended = jnp.where((shifts >> bit_index & 1)[:, None] == 1, shifted, extended)
    return extended


def live_mask(global_rows, counts, width_out, offset, bands_out):
    band_index = global_rows // width_out
    band_counts = counts[offset : offset + bands_out]
    matches = band_index[:, None] == jnp.arange(bands_out, dtype=jnp.int32)[None, :]
    live_count = jnp.sum(jnp.where(matches, band_counts[None, :], 0), axis=1)
    return global_rows % width_out < live_count


def per_device(band_state, lower_rows, upper_rows, delays, counts):
    row_count, samples = band_state.shape
    freq_index = lax.axis_index("freq")
    first_row = freq_index * row_count
    global_rows = first_row + jnp.arange(row_count, dtype=jnp.int32)
    current = band_state
    for iteration in range(ITERS):
        width_in = DMAX >> ITERS - iteration
        width_out = 2 * width_in
        bands_out = DMAX // width_out
        offset = 2**ITERS - 2 ** (ITERS - iteration)
        lower_source = lax.dynamic_slice_in_dim(lower_rows[iteration], first_row, row_count)
        upper_source = lax.dynamic_slice_in_dim(upper_rows[iteration], first_row, row_count)
        own_delays = lax.dynamic_slice_in_dim(delays[iteration], first_row, row_count)
        gathered = lax.all_gather(current, "freq", axis=0, tiled=True)
        lower_values = jnp.take(gathered, lower_source, axis=0)
        upper_values = jnp.take(gathered, upper_source, axis=0)
        rim_columns = shifted_2(upper_values[:, samples - width_in :], "tm", 1)
        extended = jnp.concatenate([rim_columns, upper_values], axis=1)
        delayed = delay_columns(extended, own_delays, width_in)[:, width_in:]
        live_rows = live_mask(global_rows, counts, width_out, offset, bands_out)
        current = jnp.where(live_rows[:, None], lower_values + delayed, jnp.zeros_like(delayed))
    return current


def solution(mesh):
    return jax.shard_map(
        per_device,
        mesh=mesh,
        in_specs=(P("freq", "tm"), P(), P(), P(), P()),
        out_specs=P("freq", "tm"),
        check_vma=False,
    )
```

profile of v0, /device:TPU:8, one launch (start us, length us, event | category | flops | bytes accessed | tf_op | source)
XLA Modules:
  0.0 244.1 jit_solution(487976752341627834)
XLA Ops:
  6.5 0.7 all-gather.4.cloned.1.call-update
  7.3 0.9 fusion.24
  8.2 0.9 fusion.23
  9.1 0.9 fusion.25
  10.1 0.7 select_reduce_fusion
  10.8 57.1 %all-gather.4.cloned.1.call-done = f32[2048,1024]{1,0:T(8,128)} async-done(((f32[128,1024]{1,0:T(8,128)}), f32[2048,1024]{1,0:T(8,128)}) %all-gather.4.cloned.1.call-update) | async-done | bytes 8388624 | tf_op jit(solution)/shard_map/all_gather | solution.py:49
  67.9 4.4 %gather_fusion.1 = f32[128,1024]{1,0:T(8,128)S(1)} fusion(f32[2048,1024]{1,0:T(8,128)} %all-gather.4.cloned.1.call-done, s32[1024]{0:T(1024)S(1)} %pad_clamp_fusion.4), kind=kCustom, calls=%fused_computation.1.clone | custom fusion | bytes 1049088 | tf_op jit(solution)/shard_map/jit(_take)/gather | solution.py:51
  72.5 3.4 %collective-permute-start = (f32[128,256]{1,0:T(8,128)S(1)}, f32[128,256]{1,0:T(8,128)S(1)}, u32[]{:S(2)}, u32[]{:S(2)}) collective-permute-start(f32[128,256]{1,0:T(8,128)S(1)} %slice.200), channel_id=1, source_target_pairs={{0,1},{1,2},{2,3},{3,4},{4,5},{5,6},{6,7},{7,8},{8,9},{9,10},{10,1... | collective-permute-start | bytes 393224 | tf_op jit(solution)/shard_map/ppermute | solution.py:13
  75.9 4.4 %gather_fusion = f32[128,1024]{1,0:T(8,128)S(1)} fusion(f32[2048,1024]{1,0:T(8,128)} %all-gather.4.cloned.1.call-done, s32[1024]{0:T(1024)S(1)} %pad_clamp_fusion.5), kind=kCustom, calls=%fused_computation.clone | custom fusion | bytes 1049088 | tf_op jit(solution)/shard_map/jit(_take)/gather | solution.py:50
  80.3 1.8 collective-permute-done
  82.2 0.3 fusion.5
  82.4 0.3 pad_select_fusion.23
  82.7 0.3 pad_select_fusion.22
  82.9 0.3 pad_select_fusion.21
  83.2 0.3 pad_select_fusion.20
  83.5 0.3 pad_select_fusion.19
  83.7 0.3 pad_select_fusion.18
  84.2 1.0 fusion.11
  85.5 52.2 %all-gather.6.cloned.1.call-done = f32[2048,1024]{1,0:T(8,128)} async-done(((f32[128,1024]{1,0:T(8,128)}), f32[2048,1024]{1,0:T(8,128)}) %all-gather.6.cloned.1.call-update) | async-done | bytes 8388624 | tf_op jit(solution)/shard_map/all_gather | solution.py:49
  137.7 4.4 %gather_fusion.3 = f32[128,1024]{1,0:T(8,128)S(1)} fusion(f32[2048,1024]{1,0:T(8,128)} %all-gather.6.cloned.1.call-done, s32[1024]{0:T(1024)S(1)} %pad_clamp_fusion.2), kind=kCustom, calls=%fused_computation.3.clone | custom fusion | bytes 1049088 | tf_op jit(solution)/shard_map/jit(_take)/gather | solution.py:51
  142.2 3.4 %collective-permute-start.1 = (f32[128,512]{1,0:T(8,128)S(1)}, f32[128,512]{1,0:T(8,128)S(1)}, u32[]{:S(2)}, u32[]{:S(2)}) collective-permute-start(f32[128,512]{1,0:T(8,128)S(1)} %slice.212), channel_id=1, source_target_pairs={{0,1},{1,2},{2,3},{3,4},{4,5},{5,6},{6,7},{7,8},{8,9},{9,10},{10,1... | collective-permute-start | bytes 786440 | tf_op jit(solution)/shard_map/ppermute | solution.py:13
  145.7 4.4 %gather_fusion.2 = f32[128,1024]{1,0:T(8,128)S(1)} fusion(f32[2048,1024]{1,0:T(8,128)} %all-gather.6.cloned.1.call-done, s32[1024]{0:T(1024)S(1)} %pad_clamp_fusion.3), kind=kCustom, calls=%fused_computation.2.clone | custom fusion | bytes 1049088 | tf_op jit(solution)/shard_map/jit(_take)/gather | solution.py:50
  150.1 4.6 %collective-permute-done.1 = f32[128,512]{1,0:T(8,128)S(1)} collective-permute-done((f32[128,512]{1,0:T(8,128)S(1)}, f32[128,512]{1,0:T(8,128)S(1)}, u32[]{:S(2)}, u32[]{:S(2)}) %collective-permute-start.1) | collective-permute-done | bytes 262176 | tf_op jit(solution)/shard_map/ppermute | solution.py:13
  154.7 0.3 fusion.3
  155.0 0.3 pad_select_fusion.16
  155.3 0.3 pad_select_fusion.15
  155.6 0.3 pad_select_fusion.14
  155.9 0.3 pad_select_fusion.13
  156.2 0.3 pad_select_fusion.12
  156.5 0.3 pad_select_fusion.11
  157.2 1.0 fusion.9
  158.2 0.6 slice.141
  158.8 51.8 %all-gather.8.cloned.1.call-done = f32[2048,1024]{1,0:T(8,128)} async-done(((f32[128,1024]{1,0:T(8,128)}), f32[2048,1024]{1,0:T(8,128)}) %all-gather.8.cloned.1.call-update) | async-done | bytes 8388624 | tf_op jit(solution)/shard_map/all_gather | solution.py:49
  210.6 4.4 %gather_fusion.5 = f32[128,1024]{1,0:T(8,128)S(1)} fusion(f32[2048,1024]{1,0:T(8,128)} %all-gather.8.cloned.1.call-done, s32[1024]{0:T(1024)S(1)} %pad_clamp_fusion), kind=kCustom, calls=%fused_computation.5.clone | custom fusion | bytes 1049088 | tf_op jit(solution)/shard_map/jit(_take)/gather | solution.py:51
  215.2 3.4 %collective-permute-start.2 = (f32[128,1024]{1,0:T(8,128)S(1)}, f32[128,1024]{1,0:T(8,128)S(1)}, u32[]{:S(2)}, u32[]{:S(2)}) collective-permute-start(f32[128,1024]{1,0:T(8,128)S(1)} %broadcast_select_fusion), channel_id=1, source_target_pairs={{0,1},{1,2},{2,3},{3,4},{4,5},{5,6},{6,7},{7,8},{8,9},{9,10},{10,1... | collective-permute-start | bytes 1572872 | tf_op jit(solution)/shard_map/ppermute | solution.py:13
  218.6 0.6 fusion.13
  219.3 4.4 %gather_fusion.4 = f32[128,1024]{1,0:T(8,128)S(1)} fusion(f32[2048,1024]{1,0:T(8,128)} %all-gather.8.cloned.1.call-done, s32[1024]{0:T(1024)S(1)} %pad_clamp_fusion.1), kind=kCustom, calls=%fused_computation.4.clone | custom fusion | bytes 1049088 | tf_op jit(solution)/shard_map/jit(_take)/gather | solution.py:50
  223.7 9.5 %collective-permute-done.2 = f32[128,1024]{1,0:T(8,128)S(1)} collective-permute-done((f32[128,1024]{1,0:T(8,128)S(1)}, f32[128,1024]{1,0:T(8,128)S(1)}, u32[]{:S(2)}, u32[]{:S(2)}) %collective-permute-start.2) | collective-permute-done | bytes 524320 | tf_op jit(solution)/shard_map/ppermute | solution.py:13
  233.3 0.4 fusion.1
  233.7 0.4 pad_select_fusion.8
  234.0 0.4 pad_select_fusion.7
  234.4 0.4 pad_select_fusion.6
  234.8 0.4 pad_select_fusion.5
  235.1 0.4 pad_select_fusion.4
  235.5 0.4 pad_select_fusion.3
  235.9 0.2 pad_select_fusion.2
  236.1 0.2 pad_select_fusion.1
  236.6 1.0 fusion.7
  (49 shorter events, 2.0 us)
Async XLA Ops:
  6.5 61.4 %all-gather.4.cloned.1.call-start = ((), (), s32[]{:S(2)}) async-start(), calls=%async_computation | async-start | bytes 8912896 | tf_op jit(solution)/shard_map/all_gather | solution.py:49
  7.3 130.4 %all-gather.6.cloned.1.call-start = ((), (), s32[]{:S(2)}) async-start(), calls=%async_computation.1 | async-start | bytes 8912896 | tf_op jit(solution)/shard_map/all_gather | solution.py:49
  72.5 9.6 %collective-permute-start = (f32[128,256]{1,0:T(8,128)S(1)}, f32[128,256]{1,0:T(8,128)S(1)}, u32[]{:S(2)}, u32[]{:S(2)}) collective-permute-start(f32[128,256]{1,0:T(8,128)S(1)} %slice.200), channel_id=1, source_target_pairs={{0,1},{1,2},{2,3},{3,4},{4,5},{5,6},{6,7},{7,8},{8,9},{9,10},{10,1... | collective-permute-start | bytes 393224 | tf_op jit(solution)/shard_map/ppermute | solution.py:13
  82.7 2.6 %copy-start = (s32[7]{0:T(128)S(1)}, s32[7]{0:T(128)}, u32[]{:S(2)}) copy-start(s32[7]{0:T(128)} %param.11) | copy-start | bytes 88
  85.2 125.4 %all-gather.8.cloned.1.call-start = ((), (), s32[]{:S(2)}) async-start(), calls=%async_computation.2 | async-start | bytes 8912896 | tf_op jit(solution)/shard_map/all_gather | solution.py:49
  142.2 12.5 %collective-permute-start.1 = (f32[128,512]{1,0:T(8,128)S(1)}, f32[128,512]{1,0:T(8,128)S(1)}, u32[]{:S(2)}, u32[]{:S(2)}) collective-permute-start(f32[128,512]{1,0:T(8,128)S(1)} %slice.212), channel_id=1, source_target_pairs={{0,1},{1,2},{2,3},{3,4},{4,5},{5,6},{6,7},{7,8},{8,9},{9,10},{10,1... | collective-permute-start | bytes 786440 | tf_op jit(solution)/shard_map/ppermute | solution.py:13
  215.2 18.1 %collective-permute-start.2 = (f32[128,1024]{1,0:T(8,128)S(1)}, f32[128,1024]{1,0:T(8,128)S(1)}, u32[]{:S(2)}, u32[]{:S(2)}) collective-permute-start(f32[128,1024]{1,0:T(8,128)S(1)} %broadcast_select_fusion), channel_id=1, source_target_pairs={{0,1},{1,2},{2,3},{3,4},{4,5},{5,6},{6,7},{7,8},{8,9},{9,10},{10,1... | collective-permute-start | bytes 1572872 | tf_op jit(solution)/shard_map/ppermute | solution.py:13
Sparse Core Ops, SparseCore 0:
  9.2 58.7 all-gather.3
  85.3 52.3 all-gather.5
  158.3 52.2 all-gather.7
where the time goes:
time: 245 us; the launch traced here: 244 us
  waiting for transfers between devices  178 us (73%)
  local copies, waits for them, and re-layouts  30.4 us (12%)
  between operations  13.6 us (6%)
  other arithmetic  12.1 us (5%)
  starting transfers between devices  10.2 us (4%)
    all_gather x3, waiting for transfers between devices, per_device(): gathered = lax.all_gather(current, 'freq', axis=0, tiled=True)  161 us
    ppermute x3, waiting for transfers between devices, shifted_2(): return lax.ppermute(block, axis, route)  15.9 us
    gather x3, local copies, waits for them, and re-layouts, per_device(): lower_values = jnp.take(gathered, lower_source, axis=0)  13.3 us
    gather x3, local copies, waits for them, and re-layouts, per_device(): upper_values = jnp.take(gathered, upper_source, axis=0)  13.3 us
    ppermute x3, starting transfers between devices, shifted_2(): return lax.ppermute(block, axis, route)  10.1 us
    select_n x27, other arithmetic, delay_columns(): jnp.where((shifts >> bit_index & 1)[:, None] == 1, shifted, extended)  7.11 us
  transfers between devices with their start and end apart: 6, of which 6 were waited for; matrix products, arithmetic and copies ran while one was open for 8% of the time, Pallas kernels for 0%

commit v1 on v0

--- a/solution.py
+++ b/solution.py
@@ -2,6 +2,7 @@
 import jax.numpy as jnp
 from jax import lax
 from jax.sharding import PartitionSpec as P
+from jax.lax import all_to_all, axis_size
 
 DMAX = 2048
 ITERS = 3
@@ -46,7 +47,10 @@
         lower_source = lax.dynamic_slice_in_dim(lower_rows[iteration], first_row, row_count)
         upper_source = lax.dynamic_slice_in_dim(upper_rows[iteration], first_row, row_count)
         own_delays = lax.dynamic_slice_in_dim(delays[iteration], first_row, row_count)
-        gathered = lax.all_gather(current, "freq", axis=0, tiled=True)
+        chips = axis_size("freq")
+        views = [chips if k == 0 else 1 for k in range(current.ndim)]
+        local_part = jnp.tile(current, views)
+        gathered = all_to_all(local_part, axis_name="freq", split_axis=0, concat_axis=0, tiled=True)
         lower_values = jnp.take(gathered, lower_source, axis=0)
         upper_values = jnp.take(gathered, upper_source, axis=0)
         rim_columns = shifted_2(upper_values[:, samples - width_in :], "tm", 1)

time: 245 us -> 647 us (2.64)
  waiting for transfers between devices: 178 us -> 568 us
  starting transfers between devices: 10.2 us -> 26.5 us
  between operations: 13.6 us -> 0.55 us
  local copies, waits for them, and re-layouts: 30.4 us -> 41.7 us
    all_to_all x0 -> x3, waiting for transfers between devices: none -> 552 us  [per_device(): all_to_all(local_part, axis_name='freq', split_axis=0, concat_axis=0, til...]
    all_gather x3 -> x0, waiting for transfers between devices: 161 us -> none  [per_device(): gathered = lax.all_gather(current, 'freq', axis=0, tiled=True)]
    all_to_all x0 -> x3, starting transfers between devices: none -> 19.1 us  [per_device(): all_to_all(local_part, axis_name='freq', split_axis=0, concat_axis=0, til...]
    another operation x0 -> x3, local copies, waits for them, and re-layouts: none -> 13.9 us  [per_device(): local_part = jnp.tile(current, views)]
  transfers between devices with their start and end apart: 6 -> 6, of which waited for: 6 -> 6; matrix products, arithmetic and copies ran while one was open for 8% -> 2% of each run, Pallas kernels for 0% -> 0%
where the time goes in v1:
time: 647 us
  waiting for transfers between devices  568 us (88%)
  local copies, waits for them, and re-layouts  41.7 us (6%)
  starting transfers between devices  26.5 us (4%)
  other arithmetic  9.88 us (2%)
    all_to_all x3, waiting for transfers between devices, per_device(): all_to_all(local_part, axis_name='freq', split_axis=0, concat_axis=0, til...  552 us
    all_to_all x3, starting transfers between devices, per_device(): all_to_all(local_part, axis_name='freq', split_axis=0, concat_axis=0, til...  19.1 us
    ppermute x3, waiting for transfers between devices, shifted_2(): return lax.ppermute(block, axis, route)  16.6 us
    another operation x3, local copies, waits for them, and re-layouts, per_device(): local_part = jnp.tile(current, views)  13.9 us
    gather x3, local copies, waits for them, and re-layouts, per_device(): lower_values = jnp.take(gathered, lower_source, axis=0)  13.3 us
    gather x3, local copies, waits for them, and re-layouts, per_device(): upper_values = jnp.take(gathered, upper_source, axis=0)  13.3 us
  transfers between devices with their start and end apart: 6, of which 6 were waited for; matrix products, arithmetic and copies ran while one was open for 2% of the time, Pallas kernels for 0%

profile of v1, /device:TPU:8, one launch (start us, length us, event | category | flops | bytes accessed | tf_op | source)
XLA Modules:
  0.0 646.7 jit_solution(9696261683808120875)
XLA Ops:
  0.0 5.3 tile.6
  5.3 8.8 %all-to-all-start = ((f32[16,128,1024]{2,1,0:T(8,128)}), f32[16,128,1024]{2,1,0:T(8,128)}, u32[]{:S(2)}, u32[]{:S(2)}) async-start(f32[16,128,1024]{2,1,0:T(8,128)} %tile.6), calls=%async_computation | async-start | bytes 16777216 | tf_op jit(solution)/shard_map/all_to_all | solution.py:53
  14.4 183.9 %all-to-all-done = f32[16,128,1024]{2,1,0:T(8,128)} async-done(((f32[16,128,1024]{2,1,0:T(8,128)}), f32[16,128,1024]{2,1,0:T(8,128)}, u32[]{:S(2)}, u32[]{:S(2)}) %all-to-all-start) | async-done | bytes 8388640 | tf_op jit(solution)/shard_map/all_to_all | solution.py:53
  198.3 4.4 gather_fusion.1
  202.9 3.4 collective-permute-start
  206.3 4.4 gather_fusion
  210.8 1.1 collective-permute-done
  211.9 0.3 fusion.5
  212.2 0.3 pad_select_fusion.23
  212.4 0.3 pad_select_fusion.22
  212.7 0.3 pad_select_fusion.21
  212.9 0.3 pad_select_fusion.20
  213.2 0.3 pad_select_fusion.19
  213.4 0.3 pad_select_fusion.18
  213.9 0.2 fusion.11
  214.1 4.3 tile.7
  218.4 5.2 all-to-all-start.1
  223.8 184.0 %all-to-all-done.1 = f32[16,128,1024]{2,1,0:T(8,128)} async-done(((f32[16,128,1024]{2,1,0:T(8,128)}), f32[16,128,1024]{2,1,0:T(8,128)}, u32[]{:S(2)}, u32[]{:S(2)}) %all-to-all-start.1) | async-done | bytes 8388640 | tf_op jit(solution)/shard_map/all_to_all | solution.py:53
  407.8 4.4 gather_fusion.3
  412.3 1.9 collective-permute-start.1
  414.3 4.4 gather_fusion.2
  418.8 5.3 collective-permute-done.1
  424.2 0.3 fusion.3
  424.4 0.3 pad_select_fusion.16
  424.7 0.3 pad_select_fusion.15
  425.0 0.3 pad_select_fusion.14
  425.3 0.3 pad_select_fusion.13
  425.6 0.3 pad_select_fusion.12
  425.9 0.3 pad_select_fusion.11
  426.6 0.2 fusion.9
  426.8 4.3 tile.8
  431.1 5.2 all-to-all-start.2
  436.3 0.6 slice.141
  436.9 183.6 %all-to-all-done.2 = f32[16,128,1024]{2,1,0:T(8,128)} async-done(((f32[16,128,1024]{2,1,0:T(8,128)}), f32[16,128,1024]{2,1,0:T(8,128)}, u32[]{:S(2)}, u32[]{:S(2)}) %all-to-all-start.2) | async-done | bytes 8388640 | tf_op jit(solution)/shard_map/all_to_all | solution.py:53
  620.5 4.4 gather_fusion.5
  625.0 2.1 collective-permute-start.2
  627.1 0.7 fusion.13
  627.9 4.4 gather_fusion.4
  632.3 10.1 %collective-permute-done.2 = f32[128,1024]{1,0:T(8,128)S(1)} collective-permute-done((f32[128,1024]{1,0:T(8,128)S(1)}, f32[128,1024]{1,0:T(8,128)S(1)}, u32[]{:S(2)}, u32[]{:S(2)}) %collective-permute-start.2) | collective-permute-done | bytes 524320 | tf_op jit(solution)/shard_map/ppermute | solution.py:14
  642.5 0.4 fusion.1
  642.9 0.4 pad_select_fusion.8
  643.2 0.4 pad_select_fusion.7
  643.6 0.4 pad_select_fusion.6
  643.9 0.4 pad_select_fusion.5
  644.3 0.4 pad_select_fusion.4
  644.6 0.4 pad_select_fusion.3
  645.1 0.2 pad_select_fusion.2
  645.8 1.0 fusion.7
  (54 shorter events, 2.2 us)
Async XLA Ops:
  5.3 8.8 %copy-start = (s32[3,2048]{1,0:T(4,128)S(1)}, s32[3,2048]{1,0:T(4,128)}, u32[]{:S(2)}) copy-start(s32[3,2048]{1,0:T(4,128)} %param.10) | copy-start | bytes 73732
  5.3 8.9 %copy-start.1 = (s32[3,2048]{1,0:T(4,128)S(1)}, s32[3,2048]{1,0:T(4,128)}, u32[]{:S(2)}) copy-start(s32[3,2048]{1,0:T(4,128)} %param.8) | copy-start | bytes 73732
  5.3 8.9 %copy-start.2 = (s32[3,2048]{1,0:T(4,128)S(1)}, s32[3,2048]{1,0:T(4,128)}, u32[]{:S(2)}) copy-start(s32[3,2048]{1,0:T(4,128)} %param.9) | copy-start | bytes 73732
  5.3 9.0 %copy-start.3 = (s32[7]{0:T(128)S(1)}, s32[7]{0:T(128)}, u32[]{:S(2)}) copy-start(s32[7]{0:T(128)} %param.11) | copy-start | bytes 88
  5.3 193.0 %all-to-all-start = ((f32[16,128,1024]{2,1,0:T(8,128)}), f32[16,128,1024]{2,1,0:T(8,128)}, u32[]{:S(2)}, u32[]{:S(2)}) async-start(f32[16,128,1024]{2,1,0:T(8,128)} %tile.6), calls=%async_computation | async-start | bytes 16777216 | tf_op jit(solution)/shard_map/all_to_all | solution.py:53
  202.9 9.0 %collective-permute-start = (f32[128,256]{1,0:T(8,128)S(1)}, f32[128,256]{1,0:T(8,128)S(1)}, u32[]{:S(2)}, u32[]{:S(2)}) collective-permute-start(f32[128,256]{1,0:T(8,128)S(1)} %slice.200), channel_id=1, source_target_pairs={{0,1},{1,2},{2,3},{3,4},{4,5},{5,6},{6,7},{7,8},{8,9},{9,10},{10,1... | collective-permute-start | bytes 393224 | tf_op jit(solution)/shard_map/ppermute | solution.py:14
  218.4 189.4 %all-to-all-start.1 = ((f32[16,128,1024]{2,1,0:T(8,128)}), f32[16,128,1024]{2,1,0:T(8,128)}, u32[]{:S(2)}, u32[]{:S(2)}) async-start(f32[16,128,1024]{2,1,0:T(8,128)} %tile.7), calls=%async_computation.1 | async-start | bytes 16777216 | tf_op jit(solution)/shard_map/all_to_all | solution.py:53
  412.3 11.8 %collective-permute-start.1 = (f32[128,512]{1,0:T(8,128)S(1)}, f32[128,512]{1,0:T(8,128)S(1)}, u32[]{:S(2)}, u32[]{:S(2)}) collective-permute-start(f32[128,512]{1,0:T(8,128)S(1)} %slice.212), channel_id=1, source_target_pairs={{0,1},{1,2},{2,3},{3,4},{4,5},{5,6},{6,7},{7,8},{8,9},{9,10},{10,1... | collective-permute-start | bytes 786440 | tf_op jit(solution)/shard_map/ppermute | solution.py:14
  431.1 189.4 %all-to-all-start.2 = ((f32[16,128,1024]{2,1,0:T(8,128)}), f32[16,128,1024]{2,1,0:T(8,128)}, u32[]{:S(2)}, u32[]{:S(2)}) async-start(f32[16,128,1024]{2,1,0:T(8,128)} %tile.8), calls=%async_computation.2 | async-start | bytes 16777216 | tf_op jit(solution)/shard_map/all_to_all | solution.py:53
  625.0 17.4 %collective-permute-start.2 = (f32[128,1024]{1,0:T(8,128)S(1)}, f32[128,1024]{1,0:T(8,128)S(1)}, u32[]{:S(2)}, u32[]{:S(2)}) collective-permute-start(f32[128,1024]{1,0:T(8,128)S(1)} %broadcast_select_fusion), channel_id=1, source_target_pairs={{0,1},{1,2},{2,3},{3,4},{4,5},{5,6},{6,7},{7,8},{8,9},{9,10},{10,1... | collective-permute-start | bytes 1572872 | tf_op jit(solution)/shard_map/ppermute | solution.py:14
